TPU v7x, 32 devices: a whole 2x2x4 slice. The times are simulated.
32 devices in a mesh: rep: 4 (over x, y), dp: 8 (over z, core).
Axes of the slice: x: 2, y: 2, z: 4, core: 2. Of those that a mesh axis runs over, the one named last changes fastest.
Arguments:
- x: bfloat16 [32, 2048, 1024], P(('rep', 'dp')), parts along dimension 0
- dy: bfloat16 [32, 2048, 1024], P(('rep', 'dp')), parts along dimension 0
- w_gate: bfloat16 [2, 1024, 4096], replicated
- w_up: bfloat16 [2, 1024, 4096], replicated
- w_down: bfloat16 [2, 4096, 1024], replicated
- m_w_gate: float32 [2, 1024, 4096], replicated
- m_w_up: float32 [2, 1024, 4096], replicated
- m_w_down: float32 [2, 4096, 1024], replicated
- v_w_gate: float32 [2, 1024, 4096], replicated
- v_w_up: float32 [2, 1024, 4096], replicated
- v_w_down: float32 [2, 4096, 1024], replicated
Outputs:
- output 1: bfloat16 [8, 1024, 4096], P('rep'), parts along dimension 0
- output 2: bfloat16 [8, 1024, 4096], P('rep'), parts along dimension 0
- output 3: bfloat16 [8, 4096, 1024], P('rep'), parts along dimension 0
- output 4: float32 [8, 1024, 4096], P('rep'), parts along dimension 0
- output 5: float32 [8, 1024, 4096], P('rep'), parts along dimension 0
- output 6: float32 [8, 4096, 1024], P('rep'), parts along dimension 0
- output 7: float32 [8, 1024, 4096], P('rep'), parts along dimension 0
- output 8: float32 [8, 1024, 4096], P('rep'), parts along dimension 0
- output 9: float32 [8, 4096, 1024], P('rep'), parts along dimension 0
There are 4 independent parts. A program takes and returns all parts, laid end to end along the dimension named above; an argument that names none is the same for every part.
All inputs are finite; a program needn't handle non-finite values.
Results may differ from a plain program's by a relative error of at most 0.0237.
Values are sent between devices in bfloat16 or wider.
A program may use at most 2.75 GiB of HBM per device.

v0:
```python
import jax
import jax.numpy as jnp
from jax import lax
from jax.sharding import PartitionSpec as P

NAMES = ("w_gate", "w_up", "w_down")


def matmul(a, w):
    return jnp.dot(a, w, preferred_element_type=jnp.float32).astype(jnp.bfloat16)


def normed(h):
    wide = h.astype(jnp.float32)
    scale = lax.rsqrt(jnp.mean(wide**2, -1, keepdims=True) + 1e-6)
    return (wide * scale).astype(jnp.bfloat16)


def layer(h, w):
    a = normed(h)
    gate = jnp.dot(a, w["w_gate"], preferred_element_type=jnp.float32)
    up = jnp.dot(a, w["w_up"], preferred_element_type=jnp.float32)
    return h + matmul((jax.nn.silu(gate) * up).astype(jnp.bfloat16), w["w_down"])


def adamw(w, m, v, g):
    m = 0.9 * m + 0.1 * g
    v = 0.95 * v + 0.05 * g * g
    step = m * lax.rsqrt(v + 1e-8) + 0.1 * w
    return (w - 0.02 * step).astype(jnp.bfloat16), m, v


def solution(mesh):
    def step(x, dy, *arrays):
        weights, m, v = (arrays[i : i + 3] for i in (0, 3, 6))
        layers = weights[0].shape[0]
        h, kept = x[0], []
        for number in range(layers):
            kept.append(h)
            h = layer(h, {name: w[number] for name, w in zip(NAMES, weights, strict=True)})
        by_h, summed = dy[0], [None] * layers
        for number in reversed(range(layers)):
            _, back = jax.vjp(lambda w, h: layer(h, w), {name: w[number] for name, w in zip(NAMES, weights, strict=True)}, kept[number])
            by_w, by_h = back(by_h)
            summed[number] = [lax.psum(by_w[name], "dp") for name in NAMES]
        gradients = [jnp.stack([summed[number][i] for number in range(layers)]).astype(jnp.float32) for i in range(3)]
        new = [adamw(w.astype(jnp.float32), m, v, g) for w, m, v, g in zip(weights, m, v, gradients, strict=True)]
        return tuple(one[which] for which in range(3) for one in new)

    return jax.shard_map(
        step,
        mesh=mesh,
        in_specs=(P(("rep", "dp"), None, None),) * 2 + (P(None, None, None),) * 9,
        out_specs=(P("rep", None, None),) * 9,
        check_vma=False,
    )
```

profile of v0, /device:TPU:0, one launch (start us, length us, event | category | flops | bytes accessed | tf_op | source)
XLA Modules:
  0.0 1601.8 jit_solution(6643812114527152447)
XLA Ops:
  7.2 0.0 all-reduce.3.cloned.1.call-start
  7.2 6.5 copy.20
  13.8 3.1 fusion.30
  16.8 0.0 copy-start.7
  16.8 6.5 copy.21
  23.4 0.0 copy-start.4
  23.4 24.5 %convolution_convert_fusion.1 = bf16[2048,4096]{1,0:T(8,128)(2,1)} fusion(bf16[2,4096,1024]{2,1,0:T(8,128)(2,1)} %param.15, bf16[1,2048,1024]{2,1,0:T(8,128)(2,1)} %param.12), kind=kOutput, calls=%fused_computation.55 | convolution fusion | flops 17188257792 | bytes 29360128 | tf_op jit(solution)/shard_map/transpose(jvp())/dot_general | solution.py:10
  47.9 0.0 copy-done.4
  47.9 23.6 %fusion.50 = f32[2048,4096]{1,0:T(8,128)} fusion(bf16[2,1024,4096]{2,1,0:T(8,128)(2,1)} %param.13, bf16[1,2048,1024]{2,1,0:T(8,128)(2,1)S(1)} %copy-done.4, f32[2048]{0:T(1024)S(1)} %add_rsqrt_fusion), kind=kOutput, calls=%fused_computation.83 | convolution fusion | flops 17186160640 | bytes 46145536 | tf_op jit(solution)/shard_map/dot_general | solution.py:21
  71.5 0.0 copy-done.7
  71.5 38.6 %multiply_convert_fusion.1 = (bf16[2048,4096]{1,0:T(8,128)(2,1)}, f32[2048,4096]{1,0:T(8,128)}) fusion(f32[2048,4096]{1,0:T(8,128)} %fusion.50, bf16[2,1024,4096]{2,1,0:T(8,128)(2,1)} %param.14, bf16[1,2048,1024]{2,1,0:T(8,128)(2,1)} %param.11, f32[2048]{0:T(1024)S(1)} %add_rsqrt_fusion), kind=kOutput, calls=%fused_computation.44 | convolution fusion | flops 17236492288 | bytes 96477184 | tf_op jit(solution)/shard_map/dot_general | solution.py:22
  110.0 23.5 %fusion.34 = (f32[2048]{0:T(1024)S(1)}, bf16[2048,1024]{0,1:T(8,128)(2,1)S(1)}) fusion(bf16[2048,4096]{1,0:T(8,128)(2,1)} %get-tuple-element.24, bf16[2,4096,1024]{2,1,0:T(8,128)(2,1)} %param.15, bf16[1,2048,1024]{1,2,0:T(8,128)(2,1)} %copy.20), kind=kOutput, calls=%fused_computation.67 | convolution fusion | flops 17190352896 | bytes 33562624 | tf_op jit(solution)/shard_map/dot_general | solution.py:10
  133.6 0.0 copy-start.5
  133.6 0.0 copy-start.2
  133.6 0.6 copy-done.5
  134.2 1.4 copy-done.2
  135.5 23.6 %fusion.37 = f32[2048,4096]{1,0:T(8,128)} fusion(bf16[2,1024,4096]{2,1,0:T(8,128)(2,1)} %param.14, bf16[2048,1024]{0,1:T(8,128)(2,1)S(1)} %get-tuple-element.27, f32[2048]{0:T(1024)S(1)} %fusion.80), kind=kOutput, calls=%fused_computation.70 | convolution fusion | flops 17186160640 | bytes 46145536 | tf_op jit(solution)/shard_map/jvp()/dot_general | solution.py:22
  159.1 46.6 %fusion.14 = (bf16[2048,4096]{1,0:T(8,128)(2,1)}, f32[2048,4096]{1,0:T(8,128)}) fusion(f32[2048,4096]{1,0:T(8,128)} %fusion.37, bf16[2048,4096]{1,0:T(8,128)(2,1)} %convolution_convert_fusion.1, bf16[2,1024,4096]{2,1,0:T(8,128)(2,1)} %param.13, bf16[2048,1024]{0,1:T(8,128)(2,1)} %copy-done.2, f32[2048]{0:T(1024)S(1)} %fusion.80), kind=kOutput, calls=%fused_computation.32 | convolution fusion | flops 17286823936 | bytes 113254400 | tf_op jit(solution)/shard_map/jvp()/dot_general | solution.py:21
  205.7 27.1 %fusion.27 = bf16[2048,1024]{0,1:T(8,128)(2,1)} fusion(bf16[2048,4096]{1,0:T(8,128)(2,1)} %convolution_convert_fusion.1, bf16[2,1024,4096]{2,1,0:T(8,128)(2,1)} %param.14, f32[2048,4096]{1,0:T(8,128)} %get-tuple-element.29), kind=kOutput, calls=%fused_computation.48 | convolution fusion | flops 17230200832 | bytes 62914560 | tf_op jit(solution)/shard_map/transpose(jvp())/dot_general | solution.py:22
  232.9 26.7 %convert_bitcast_fusion.2 = bf16[1,1024,4096]{2,1,0:T(8,128)(2,1)} fusion(bf16[2048,4096]{1,0:T(8,128)(2,1)} %convolution_convert_fusion.1, bf16[2048,1024]{0,1:T(8,128)(2,1)} %copy-done.2, f32[2048]{0:T(1024)S(1)} %fusion.80, f32[2048,4096]{1,0:T(8,128)} %get-tuple-element.29), kind=kOutput, calls=%fused_computation.87 | convolution fusion | flops 17240686592 | bytes 62922752 | tf_op jit(solution)/shard_map/transpose(jvp())/dot_general | solution.py:22
  259.5 0.0 copy-start.3
  259.5 30.9 %convert_bitcast_fusion = bf16[1,4096,1024]{2,1,0:T(8,128)(2,1)} fusion(f32[2048,4096]{1,0:T(8,128)} %fusion.37, bf16[1,2048,1024]{2,1,0:T(8,128)(2,1)} %param.12, f32[2048,4096]{1,0:T(8,128)} %get-tuple-element.29), kind=kOutput, calls=%fused_computation.85 | convolution fusion | flops 17234395136 | bytes 79691776 | tf_op jit(solution)/shard_map/transpose(jvp())/dot_general | solution.py:10
  290.5 0.0 copy-done.3
  290.5 21.6 %convert_bitcast_fusion.4 = bf16[1,1024,4096]{2,1,0:T(8,128)(2,1)} fusion(bf16[2048,4096]{1,0:T(8,128)(2,1)} %get-tuple-element.28, bf16[2048,1024]{0,1:T(8,128)(2,1)S(1)} %copy-done.3, f32[2048]{0:T(1024)S(1)} %fusion.80), kind=kOutput, calls=%fused_computation.89 | convolution fusion | flops 17186160640 | bytes 29368320 | tf_op jit(solution)/shard_map/transpose(jvp())/dot_general | solution.py:21
  312.1 0.0 copy-start.6
  312.1 0.0 copy-start
  312.1 25.4 %fusion.36 = (f32[2048]{0:T(1024)S(1)}, bf16[2048,1024]{0,1:T(8,128)(2,1)}) fusion(bf16[2048,1024]{0,1:T(8,128)(2,1)S(1)} %copy-done.3, bf16[2048,1024]{0,1:T(8,128)(2,1)} %fusion.27, bf16[2048,4096]{1,0:T(8,128)(2,1)} %get-tuple-element.28, bf16[2,1024,4096]{2,1,0:T(8,128)(2,1)} %param.13), kind=kOutput, calls=%fused_computation.69 | convolution fusion | flops 17190352896 | bytes 37756928 | tf_op jit(solution)/shard_map/transpose(jvp())/dot_general | solution.py:21
  337.5 0.0 copy-done.6
  337.5 0.0 copy-done
  337.5 6.0 fusion.65
  343.5 25.0 %convolution_convert_fusion = bf16[2048,4096]{1,0:T(8,128)(2,1)} fusion(bf16[2048,1024]{0,1:T(8,128)(2,1)} %fusion.65, bf16[2,4096,1024]{2,1,0:T(8,128)(2,1)} %param.15), kind=kOutput, calls=%fused_computation.54 | convolution fusion | flops 17188257792 | bytes 29360128 | tf_op jit(solution)/shard_map/transpose(jvp())/dot_general | solution.py:10
  368.5 0.0 copy-start.1
  368.5 0.0 copy-start.8
  368.5 24.4 %convert_bitcast_fusion.1 = bf16[1,4096,1024]{2,1,0:T(8,128)(2,1)} fusion(bf16[2048,4096]{1,0:T(8,128)(2,1)} %get-tuple-element.24, bf16[2048,1024]{0,1:T(8,128)(2,1)} %fusion.65), kind=kOutput, calls=%fused_computation.86 | convolution fusion | flops 17184063488 | bytes 29360128 | tf_op jit(solution)/shard_map/transpose(jvp())/dot_general | solution.py:10
  392.9 0.0 copy-done.1
  392.9 0.0 copy-done.8
  392.9 25.5 %convert_bitcast_fusion.3 = bf16[1,1024,4096]{2,1,0:T(8,128)(2,1)} fusion(bf16[2048,4096]{1,0:T(8,128)(2,1)} %convolution_convert_fusion, f32[2048,4096]{1,0:T(8,128)} %fusion.50, bf16[1,2048,1024]{1,2,0:T(8,128)(2,1)S(1)} %copy-done.1, f32[2048]{0:T(1024)S(1)} %copy-done.8), kind=kOutput, calls=%fused_computation.88 | convolution fusion | flops 17240686592 | bytes 62922752 | tf_op jit(solution)/shard_map/transpose(jvp())/dot_general | solution.py:22
  418.4 37.1 %convert_bitcast_fusion.5 = bf16[1,1024,4096]{2,1,0:T(8,128)(2,1)} fusion(f32[2048,4096]{1,0:T(8,128)} %fusion.50, f32[2048,4096]{1,0:T(8,128)} %get-tuple-element.25, bf16[2048,4096]{1,0:T(8,128)(2,1)} %convolution_convert_fusion, bf16[1,2048,1024]{1,2,0:T(8,128)(2,1)} %copy.20, f32[2048]{0:T(1024)S(1)} %copy-done.8), kind=kOutput, calls=%fused_computation.90 | convolution fusion | flops 17282629632 | bytes 96477184 | tf_op jit(solution)/shard_map/transpose(jvp())/dot_general | solution.py:21
  455.5 0.0 all-reduce.3.cloned.1.call-update
  455.5 965.2 %all-reduce.3.cloned.1.call-done = (bf16[1,1024,4096]{2,1,0:T(8,128)(2,1)}, bf16[1,1024,4096]{2,1,0:T(8,128)(2,1)}, bf16[1,1024,4096]{2,1,0:T(8,128)(2,1)}, bf16...) async-done(((bf16[1,1024,4096]{2,1,0:T(8,128)(2,1)}, bf16[1,1024,4096]{2,1,0:T(8,128)(2,1)}, ...) | async-done | bytes 50331664 | tf_op jit(solution)/shard_map/psum | solution.py:45
  1420.7 57.5 %fusion.11 = (bf16[2,4096,1024]{2,1,0:T(8,128)(2,1)}, f32[2,4096,1024]{2,1,0:T(8,128)}, f32[2,4096,1024]{2,1,0:T(8,128)}) fusion(bf16[2,4096,1024]{2,1,0:T(8,128)(2,1)} %param.15, bf16[1,4096,1024]{2,1,0:T(8,128)(2,1)} %get-tuple-element.13, bf16[1,4096,1024]{2,1,0:T(8,128)(2,1)} %get-tuple-element.14, f32[2,4096,1024]{2,1,0:T(8,128)} %param.21, ...), kind=kLoop, calls=%fused_computation.29 | loop fusion | flops 159383552 | bytes 184549376 | tf_op jit(solution)/shard_map/convert_element_type | solution.py:30
  1478.2 116.2 %fusion.2 = (bf16[2,1024,4096]{2,1,0:T(8,128)(2,1)}, f32[2,1024,4096]{2,1,0:T(8,128)}, f32[2,1024,4096]{2,1,0:T(8,128)}, bf16[2,1024,4096]{2,1,0:T(8,128)(2,1)},...) fusion(bf16[2,1024,4096]{2,1,0:T(8,128)(2,1)} %param.13, bf16[1,1024,4096]{2,1,0:T(8,128)(2,1)} %get-tuple-element.9, ...), kind=kLoop, calls=%fused_computation.20 | loop fusion | flops 318767104 | bytes 369098752 | tf_op jit(solution)/shard_map/convert_element_type | solution.py:30
  (3 shorter events, 0.0 us)
Async XLA Ops:
  7.2 1413.5 %all-reduce.3.cloned.1.call-start = ((), (), s32[]{:S(2)}) async-start(), calls=%async_computation | async-start | bytes 100663296 | tf_op jit(solution)/shard_map/psum | solution.py:45
  16.8 54.6 %copy-start.7 = (f32[2048]{0:T(1024)}, f32[2048]{0:T(1024)S(1)}, u32[]{:S(2)}) copy-start(f32[2048]{0:T(1024)S(1)} %add_rsqrt_fusion) | copy-start | bytes 24580
  23.4 24.5 %copy-start.4 = (bf16[1,2048,1024]{2,1,0:T(8,128)(2,1)S(1)}, bf16[1,2048,1024]{2,1,0:T(8,128)(2,1)}, u32[]{:S(2)}) copy-start(bf16[1,2048,1024]{2,1,0:T(8,128)(2,1)} %param.11) | copy-start | bytes 12582916
  133.6 0.6 copy-start.5
  133.6 2.0 copy-start.2
  259.5 30.9 %copy-start.3 = (bf16[2048,1024]{0,1:T(8,128)(2,1)S(1)}, bf16[2048,1024]{0,1:T(8,128)(2,1)}, u32[]{:S(2)}) copy-start(bf16[2048,1024]{0,1:T(8,128)(2,1)} %copy-done.2) | copy-start | bytes 12582916
  312.1 25.4 %copy-start.6 = (f32[2048]{0:T(1024)S(1)}, f32[2048]{0:T(1024)}, u32[]{:S(2)}) copy-start(f32[2048]{0:T(1024)} %copy-done.5) | copy-start | bytes 24580
  312.1 25.4 %copy-start = (bf16[1,2048,1024]{1,2,0:T(8,128)(2,1)S(1)}, bf16[1,2048,1024]{1,2,0:T(8,128)(2,1)}, u32[]{:S(2)}) copy-start(bf16[1,2048,1024]{1,2,0:T(8,128)(2,1)} %copy.21) | copy-start | bytes 12582916
  368.5 24.4 %copy-start.1 = (bf16[1,2048,1024]{1,2,0:T(8,128)(2,1)S(1)}, bf16[1,2048,1024]{1,2,0:T(8,128)(2,1)}, u32[]{:S(2)}) copy-start(bf16[1,2048,1024]{1,2,0:T(8,128)(2,1)} %copy.20) | copy-start | bytes 12582916
  368.5 24.4 %copy-start.8 = (f32[2048]{0:T(1024)S(1)}, f32[2048]{0:T(1024)}, u32[]{:S(2)}) copy-start(f32[2048]{0:T(1024)} %copy-done.7) | copy-start | bytes 24580
Sparse Core Ops, SparseCore 0:
  455.7 964.9 all-reduce.2
where the time goes:
time: 1610 us; the launch traced here: 1600 us
  waiting for transfers between devices  965 us (60%)
  matrix products  424 us (26%)
  other arithmetic  183 us (11%)
    psum x1, waiting for transfers between devices, step(): summed[number] = [lax.psum(by_w[name], 'dp') for name in NAMES]  965 us
    convert_element_type x2, other arithmetic, adamw(): return ((w - 0.02 * step).astype(jnp.bfloat16), m, v)  174 us
    dot_general x5, matrix products, layer(): gate = jnp.dot(a, w['w_gate'], preferred_element_type=jnp.float32)  154 us
    dot_general x5, matrix products, layer(): up = jnp.dot(a, w['w_up'], preferred_element_type=jnp.float32)  141 us
    dot_general x5, matrix products, matmul(): jnp.dot(a, w, preferred_element_type=jnp.float32).astype(jnp.bfloat16)  128 us
  transfers between devices with their start and end apart: 1, of which 1 were waited for; matrix products, arithmetic and copies ran while one was open for 0% of the time, Pallas kernels for 0%

commit v1 on v0

v1 whole, which is shorter than its diff:
```python
import jax
import jax.numpy as jnp
from jax import lax
from jax.experimental import pallas as pl
from jax.experimental.pallas import tpu as pltpu
from jax.sharding import PartitionSpec as P

F32 = jnp.float32
BF16 = jnp.bfloat16
T, D, FF = 2048, 1024, 4096
C = 256
J = FF // C
N = 6 * J
K = 12
HALF, QUARTER = D // 2, D // 4
ROWS = 1024
S1, S2, S3, S4, S5, S6, S7 = 1, 3, 5, 7, 9, 10, 11
NN = (((1,), (0,)), ((), ()))
NT = (((1,), (1,)), ((), ()))


def dot(a, b, dims=NN):
    return lax.dot_general(a, b, dims, preferred_element_type=F32)


def normalised(h):
    wide = h.astype(F32)
    return (wide * lax.rsqrt(jnp.mean(wide * wide, -1, keepdims=True) + 1e-6)).astype(BF16)


def tiles(total, size, body):
    @pl.loop(0, total // size)
    def _(i):
        body(pl.ds(pl.multiple_of(i * size, size), size))


def mega(x, dy, wg, wu, wd, h1, gs, a, at, dh, dht, acc, wgb, wub, wdb, act, dg, du, g, r0, r1, r2, full, wsem, csem, osem, *sems):
    s0s, s0r, s1s, s1r, s2s, s2r, s3s, s3r, s4s, s4r, s5s, s5r, s6s, s6r = sems
    me = lax.axis_index("dp")
    z, c = me // 2, me % 2
    end = (z == 0) | (z == 3)
    mid = (z == 1) | (z == 2)
    partner = 2 * z + (1 - c)
    inward = jnp.where(z == 0, 1, jnp.where(z == 1, 2, jnp.where(z == 2, 1, 2))) * 2 + c
    outward = jnp.where(z == 1, 0, 3) * 2 + c
    barrier = pltpu.get_barrier_semaphore()

    def hello(device):
        pl.semaphore_signal(barrier, inc=1, device_id={"dp": device}, device_id_type=pl.DeviceIdType.MESH)

    hello(partner)
    hello(inward)

    @pl.when(mid)
    def _():
        hello(outward)
        pl.semaphore_wait(barrier, 3)

    @pl.when(end)
    def _():
        pl.semaphore_wait(barrier, 2)

    def remote(src, dst, send, recv, device):
        return pltpu.make_async_remote_copy(
            src_ref=src, dst_ref=dst, send_sem=send, recv_sem=recv, device_id={"dp": device}, device_id_type=pl.DeviceIdType.MESH
        )

    def local(src, dst, sem):
        return pltpu.make_async_copy(src, dst, sem)

    def fetch(u):
        layer = jnp.where(u // J == 1, 1, 0)
        cols = pl.ds(pl.multiple_of(u % J * C, C), C)
        slot = u % 2
        return (
            local(wg.at[layer, :, cols], wgb.at[slot], wsem.at[0, slot]),
            local(wu.at[layer, :, cols], wub.at[slot], wsem.at[1, slot]),
            local(wd.at[layer, cols, :], wdb.at[slot], wsem.at[2, slot]),
        )

    def next_weights(u):
        @pl.when(u + 1 < 3 * J)
        def _():
            for copy in fetch(u + 1):
                copy.start()

        for copy in fetch(u):
            copy.wait()

    mine, other = c * HALF, (1 - c) * HALF
    own, away = (2 - z) * QUARTER, (z - 1) * QUARTER

    def at_row(row, size):
        return pl.ds(pl.multiple_of(row, QUARTER), size)

    def stage0(n):
        s = n % K
        return remote(g.at[s, at_row(other, HALF)], r0.at[s], s0s.at[s], s0r.at[s], partner)

    def stage1(n):
        s = n % K
        return remote(g.at[s, at_row(mine, HALF)], r1.at[s], s1s.at[s], s1r.at[s], inward)

    def stage2(n):
        s = n % K
        return remote(g.at[s, at_row(mine + away, QUARTER)], r2.at[s], s2s.at[s], s2r.at[s], inward)

    def stage3(n):
        s = n % K
        rows = full.at[s, at_row(mine + own, QUARTER)]
        return remote(rows, rows, s3s.at[s], s3r.at[s], inward)

    def stage4(n, row):
        s = n % K
        rows = full.at[s, at_row(row, QUARTER)]
        return remote(rows, rows, s4s.at[s], s4r.at[s], outward)

    def stage5(n, row):
        s = n % K
        rows = full.at[s, at_row(row, QUARTER)]
        return remote(rows, rows, s5s.at[s], s5r.at[s], outward)

    def stage6(n):
        s = n % K
        rows = full.at[s, at_row(mine, HALF)]
        return remote(rows, rows, s6s.at[s], s6r.at[s], partner)

    def result(n):
        s = n % K
        cols = pl.ds(pl.multiple_of(n // 3 % J * C, C), C)
        return local(full.at[s], gs.at[1 - n // (3 * J), n % 3, :, cols], osem.at[s])

    def live(n, also=None):
        ok = (n >= 0) & (n < N)
        return ok if also is None else ok & also

    def tick(t):
        @pl.when(live(t - S7))
        def _():
            result(t - S7).wait()

        @pl.when(live(t - S1))
        def _():
            n = t - S1
            s = n % K
            stage0(n).wait_recv()
            rows = at_row(mine, HALF)
            g[s, rows] = (g[s, rows].astype(F32) + r0[s].astype(F32)).astype(BF16)

            @pl.when(end)
            def _():
                stage1(n).start()

        @pl.when(live(t - S4, mid))
        def _():
            n = t - S4
            stage3(n).wait_recv()
            stage5(n, mine + away).start()

        @pl.when(live(t - S3, mid))
        def _():
            n = t - S3
            s = n % K
            stage2(n).wait()
            rows = at_row(mine + own, QUARTER)
            r = at_row(own, QUARTER)
            full[s, rows] = (g[s, rows].astype(F32) + r1[s, r].astype(F32) + r2[s].astype(F32)).astype(BF16)
            stage3(n).start()
            stage4(n, mine + own).start()

        @pl.when(live(t - S3, end))
        def _():
            stage1(t - S3).wait_send()

        @pl.when(live(t - S2, mid))
        def _():
            n = t - S2
            s = n % K
            stage1(n).wait_recv()
            rows = at_row(mine + away, QUARTER)
            g[s, rows] = (g[s, rows].astype(F32) + r1[s, at_row(away, QUARTER)].astype(F32)).astype(BF16)
            stage2(n).start()

        @pl.when(live(t - S2))
        def _():
            stage0(t - S2).wait_send()

        @pl.when(live(t - S5, end))
        def _():
            n = t - S5
            stage4(n, mine).wait_recv()
            stage5(n, mine).wait_recv()

        @pl.when(live(t - S5, mid))
        def _():
            n = t - S5
            stage3(n).wait_send()
            stage4(n, mine).wait_send()
            stage5(n, mine).wait_send()

        @pl.when(live(t - S5))
        def _():
            stage6(t - S5).start()

        @pl.when(live(t))
        def _():
            stage0(t).start()

        @pl.when(live(t - S6))
        def _():
            n = t - S6
            stage6(n).wait()
            result(n).start()

    for copy in fetch(0):
        copy.start()
    into_a = local(x.at[0], a, csem.at[0])
    into_dh = local(x.at[0], dh, csem.at[1])
    into_a.start()
    into_dh.start()
    into_a.wait()

    def norm_rows(s):
        a[s] = normalised(a[s])

    tiles(T, 256, norm_rows)
    acc[...] = jnp.zeros_like(acc)

    @pl.loop(0, J)
    def _(u):
        next_weights(u)
        slot = u % 2

        def rows(s):
            gate, up = dot(a[s], wgb[slot]), dot(a[s], wub[slot])
            act[s] = (gate * jax.nn.sigmoid(gate) * up).astype(BF16)
            acc[s] += dot(act[s], wdb[slot])

        tiles(T, ROWS, rows)

    into_dh.wait()

    def first_states(s):
        h = (dh[s].astype(F32) + acc[s].astype(BF16).astype(F32)).astype(BF16)
        dh[s] = h
        a[s] = normalised(h)
        acc[s] = jnp.zeros_like(acc[s])

    tiles(T, 256, first_states)
    keep = local(dh, h1, csem.at[0])
    keep.start()

    def turn(source, target):
        def cols(s):
            target[s] = source[:, s].T

        tiles(D, 256, cols)

    turn(a, at)
    keep.wait()
    into_dh = local(dy.at[0], dh, csem.at[1])
    into_dh.start()
    into_dh.wait()
    turn(dh, dht)

    @pl.loop(0, 2 * J)
    def _(it):
        next_weights(J + it)
        slot = it % 2

        @pl.when(it == J)
        def _():
            again = local(h1, a, csem.at[0])
            again.start()
            again.wait()

            def rows(s):
                wide = a[s].astype(F32)
                d = acc[s].astype(BF16).astype(F32)
                scale = lax.rsqrt(jnp.mean(wide * wide, -1, keepdims=True) + 1e-6)
                along = jnp.sum(d * wide, -1, keepdims=True)
                d = (scale * d - wide * (scale * scale * scale * (1.0 / D) * along)).astype(BF16)
                dh[s] = (dh[s].astype(F32) + d.astype(F32)).astype(BF16)

            tiles(T, 256, rows)
            again = local(x.at[0], a, csem.at[0])
            again.start()
            turn(dh, dht)
            again.wait()
            tiles(T, 256, norm_rows)
            turn(a, at)

        def rows(s):
            gate, up = dot(a[s], wgb[slot]), dot(a[s], wub[slot])
            d = dot(dh[s], wdb[slot], NT).astype(BF16).astype(F32)
            sig = jax.nn.sigmoid(gate)
            silu = gate * sig
            act[s] = (silu * up).astype(BF16)
            du[s] = (d * silu).astype(BF16)
            dg[s] = (d * up * (sig * (1.0 + gate * (1.0 - sig)))).astype(BF16)

        tiles(T, ROWS, rows)
        tick(3 * it - 1)
        base = it % 4 * 3
        g[base] = dot(dht[...], act[...]).astype(BF16)
        g[base + 1] = dot(at[...], dg[...]).astype(BF16)
        g[base + 2] = dot(at[...], du[...]).astype(BF16)
        tick(3 * it)

        @pl.when(it < J)
        def _():
            def rows(s):
                acc[s] += dot(dg[s], wgb[slot], NT) + dot(du[s], wub[slot], NT)

            tiles(T, ROWS, rows)

        tick(3 * it + 1)

    @pl.loop(N - 1, N + S7)
    def _(t):
        tick(t)


def gradients(x, dy, wg, wu, wd):
    anywhere = pl.BlockSpec(memory_space=pl.ANY)
    sem = pltpu.SemaphoreType.DMA
    vm = pltpu.VMEM
    return pl.pallas_call(
        mega,
        out_shape=(jax.ShapeDtypeStruct((T, D), BF16), jax.ShapeDtypeStruct((2, 3, D, FF), BF16)),
        in_specs=[anywhere] * 5,
        out_specs=(anywhere, anywhere),
        scratch_shapes=[
            vm((T, D), BF16), vm((D, T), BF16), vm((T, D), BF16), vm((D, T), BF16), vm((T, D), F32),
            vm((2, D, C), BF16), vm((2, D, C), BF16), vm((2, C, D), BF16),
            vm((T, C), BF16), vm((T, C), BF16), vm((T, C), BF16),
            vm((K, D, C), BF16), vm((K, HALF, C), BF16), vm((K, HALF, C), BF16), vm((K, QUARTER, C), BF16), vm((K, D, C), BF16),
            sem((3, 2)), sem((2,)), sem((K,)),
        ] + [sem((K,))] * 14,
        compiler_params=pltpu.CompilerParams(collective_id=0, has_side_effects=True, vmem_limit_bytes=67043328),
        name="gradients",
    )(x, dy, wg, wu, wd)


def adam_body(turned, g, w, m, v, ow, om, ov):
    gg = g[0, 0].T if turned else g[0, 0]
    gg = gg.astype(F32)
    mm = 0.9 * m[0] + 0.1 * gg
    vv = 0.95 * v[0] + 0.05 * gg * gg
    ww = w[0].astype(F32)
    ow[0] = (ww - 0.02 * (mm * lax.rsqrt(vv + 1e-8) + 0.1 * ww)).astype(BF16)
    om[0] = mm
    ov[0] = vv


def adam(which, gs, w, m, v):
    down = which == 0
    if down:
        rows, cols = 256, D
        gspec = pl.BlockSpec((1, 1, D, rows), lambda l, i: (l, which, 0, i))
    else:
        rows, cols = 64, FF
        gspec = pl.BlockSpec((1, 1, rows, FF), lambda l, i: (l, which, i, 0))
    spec = pl.BlockSpec((1, rows, cols), lambda l, i: (l, i, 0))
    return pl.pallas_call(
        lambda *refs: adam_body(down, *refs),
        grid=(2, w.shape[1] // rows),
        in_specs=[gspec, spec, spec, spec],
        out_specs=[spec] * 3,
        out_shape=[jax.ShapeDtypeStruct(w.shape, t) for t in (BF16, F32, F32)],
        name="adam",
    )(gs, w, m, v)


def solution(mesh):
    def step(x, dy, wg, wu, wd, mg, mu, md, vg, vu, vd):
        _, gs = gradients(x, dy, wg, wu, wd)
        new = [adam(1, gs, wg, mg, vg), adam(2, gs, wu, mu, vu), adam(0, gs, wd, md, vd)]
        return tuple(new[i][which] for which in range(3) for i in range(3))

    return jax.shard_map(
        step,
        mesh=mesh,
        in_specs=(P(("rep", "dp"), None, None),) * 2 + (P(None, None, None),) * 9,
        out_specs=(P("rep", None, None),) * 9,
        check_vma=False,
    )
```

time: 1610 us -> 872 us (0.54)
  waiting for transfers between devices: 965 us -> 0 us
  Pallas kernels: 0 us -> 871 us
  matrix products: 424 us -> 0 us
  other arithmetic: 183 us -> 0 us
    psum x1 -> x0, waiting for transfers between devices: 965 us -> none  [step(): summed[number] = [lax.psum(by_w[name], 'dp') for name in NAMES]]
    pallas_call x0 -> x4, Pallas kernels: none -> 871 us  [the longest x1 661 us: gradients(): pl.pallas_call(mega, out_shape=(jax.ShapeDtypeStruct((T, D), BF16), jax.S...]
    dot_general x15 -> x0, matrix products: 424 us -> none  [the longest x5 154 us: layer(): gate = jnp.dot(a, w['w_gate'], preferred_element_type=jnp.float32)]
    convert_element_type x2 -> x0, other arithmetic: 174 us -> none  [adamw(): return ((w - 0.02 * step).astype(jnp.bfloat16), m, v)]
  transfers between devices with their start and end apart: 1 -> 0, of which waited for: 1 -> 0; matrix products, arithmetic and copies ran while one was open for 0% -> 0% of each run, Pallas kernels for 0% -> 0%
where the time goes in v1:
time: 872 us
  Pallas kernels  871 us (100%)
    pallas_call x1, Pallas kernels, gradients(): pl.pallas_call(mega, out_shape=(jax.ShapeDtypeStruct((T, D), BF16), jax.S...  661 us
    pallas_call x3, Pallas kernels, adam(): pl.pallas_call(lambda *refs: adam_body(down, *refs), grid=(2, w.shape[1]...  210 us

profile of v1, /device:TPU:0, one launch (start us, length us, event | category | flops | bytes accessed | tf_op | source)
XLA Modules:
  0.0 871.8 jit_solution(1064195460469844601)
XLA Ops:
  0.6 661.4 %gradients.1 = (bf16[2048,1024]{1,0:T(8,128)(2,1)}, bf16[2,3,1024,4096]{3,2,1,0:T(8,128)(2,1)}) custom-call(bf16[1,2048,1024]{2,1,0:T(8,128)(2,1)} %x.1, bf16[1,2048,1024]{2,1,0:T(8,128)(2,1)} %dy.1, bf16[2,1024,4096]{2,1,0:T(8,128)(2,1)} %refs_1_.3, bf16[2,1024,4096]{2,1,0:T(8,128)(2,1)} %refs_1_.4, bf16[2,4096,1024]{2,1,0:T(8,128)(2,1)} %refs_1_.5), custom_call_target="tpu_custom_call" | custom-call | tf_op jit(solution)/shard_map/gradients/pallas_call | solution.py:328
  662.1 71.8 %adam.5 = (bf16[2,4096,1024]{2,1,0:T(8,128)(2,1)}, f32[2,4096,1024]{2,1,0:T(8,128)}, f32[2,4096,1024]{2,1,0:T(8,128)}) custom-call(bf16[2,3,1024,4096]{3,2,1,0:T(8,128)(2,1)} %get-tuple-element.19.refs_0_, bf16[2,4096,1024]{2,1,0:T(8,128)(2,1)} %refs_1_.5, f32[2,4096,1024]{2,1,0:T(8,128)} %refs_2_.5, f32[2,4096,1024]{2,1,0:T(8,128)} %refs_3_.5), custom_call_target="tpu_custom_call" | custom-call | tf_op jit(solution)/shard_map/adam/pallas_call | solution.py:365
  733.9 68.9 %adam.4 = (bf16[2,1024,4096]{2,1,0:T(8,128)(2,1)}, f32[2,1024,4096]{2,1,0:T(8,128)}, f32[2,1024,4096]{2,1,0:T(8,128)}) custom-call(bf16[2,3,1024,4096]{3,2,1,0:T(8,128)(2,1)} %get-tuple-element.19.refs_0_, bf16[2,1024,4096]{2,1,0:T(8,128)(2,1)} %refs_1_.4, f32[2,1024,4096]{2,1,0:T(8,128)} %refs_2_.4, f32[2,1024,4096]{2,1,0:T(8,128)} %refs_3_.4), custom_call_target="tpu_custom_call" | custom-call | tf_op jit(solution)/shard_map/adam/pallas_call | solution.py:365
  802.8 68.9 %adam.3 = (bf16[2,1024,4096]{2,1,0:T(8,128)(2,1)}, f32[2,1024,4096]{2,1,0:T(8,128)}, f32[2,1024,4096]{2,1,0:T(8,128)}) custom-call(bf16[2,3,1024,4096]{3,2,1,0:T(8,128)(2,1)} %get-tuple-element.19.refs_0_, bf16[2,1024,4096]{2,1,0:T(8,128)(2,1)} %refs_1_.3, f32[2,1024,4096]{2,1,0:T(8,128)} %refs_2_.3, f32[2,1024,4096]{2,1,0:T(8,128)} %refs_3_.3), custom_call_target="tpu_custom_call" | custom-call | tf_op jit(solution)/shard_map/adam/pallas_call | solution.py:365
